TPU v7x, 32 devices: a whole 2x2x4 slice. The times are simulated.
32 devices in a mesh: fsdp: 8 (over z, y), dp: 4 (over x, core).
Axes of the slice: x: 2, y: 2, z: 4, core: 2. Of those that a mesh axis runs over, the one named last changes fastest.
Arguments:
- tokens: bfloat16 [512, 4096], P('dp', 'fsdp'), may hold values from -6 to 6
- out_grad: bfloat16 [512, 5120], P('dp', 'fsdp'), may hold values from -0.26367188 to 0.26367188
- master: float32 [4096, 5120], P('fsdp'), may hold values from -0.09375 to 0.09375
- moment_one: float32 [4096, 5120], P('fsdp'), may hold values from -3 to 3
- moment_two: float32 [4096, 5120], P('fsdp'), may hold values from 0.1 to 4
- flags: int32 [32, 16], P(('fsdp', 'dp')), may hold values 0 or 1
- steps: int32 [16], replicated, may hold values from 1 to 8
- rate: float32 [1], replicated, may hold values from 0.001 to 0.01
Outputs:
- master_next: float32 [4096, 5120], P('fsdp')
- moment_one_next: float32 [4096, 5120], P('fsdp')
- moment_two_next: float32 [4096, 5120], P('fsdp')
- weight_half: bfloat16 [4096, 5120], P('fsdp')
- steps_next: int32 [16], replicated
- outputs: bfloat16 [512, 5120], P('dp', 'fsdp')
All inputs are finite; a program needn't handle non-finite values. No bound on the sum of `flags` on one device may be relied on, other than what follows from the above.
Results may differ from a plain program's by a relative error of at most 0.0049.
Values may be sent and summed in bfloat16 or wider, within the bound.
A program may use at most 128 MiB of HBM per device.

v0:
```python
import jax
import jax.numpy as jnp
from jax import lax
from jax.sharding import PartitionSpec as P

BUCKETS = 16
first_decay = 0.9
second_decay = 0.95
epsilon = 1e-08


def local(tokens, out_grad, master, moment_one, moment_two, flags, steps, rate):
    width_out = master.shape[1]
    bucket_width = width_out // BUCKETS
    contract_rows = (((0,), (0,)), ((), ()))
    rows = lax.all_gather(tokens, "dp", axis=0, tiled=True)
    grads = lax.all_gather(
        lax.all_gather(out_grad, "fsdp", axis=1, tiled=True), "dp", axis=0, tiled=True
    )
    counts = lax.psum(flags[0], ("fsdp", "dp"))
    gradient = lax.dot_general(rows, grads, contract_rows, preferred_element_type=jnp.float32)
    commit_bucket = counts == 0
    commit = jnp.repeat(commit_bucket, bucket_width)[None, :]
    times = jnp.repeat(steps + 1, bucket_width).astype(jnp.float32)[None, :]
    first = first_decay * moment_one + (1.0 - first_decay) * gradient
    second = second_decay * moment_two + (1.0 - second_decay) * gradient * gradient
    fix_one = 1.0 - jnp.power(jnp.float32(first_decay), times)
    fix_two = 1.0 - jnp.power(jnp.float32(second_decay), times)
    candidate = master - rate[0] * (first / fix_one) / (jnp.sqrt(second / fix_two) + epsilon)
    master_next = jnp.where(commit, candidate, master)
    moment_one_next = jnp.where(commit, first, moment_one)
    moment_two_next = jnp.where(commit, second, moment_two)
    weight_half = master_next.astype(jnp.bfloat16)
    steps_next = steps + commit_bucket.astype(jnp.int32)
    share = lax.dot_general(
        tokens, weight_half, (((1,), (0,)), ((), ())), preferred_element_type=jnp.float32
    ).astype(jnp.bfloat16)
    shards = lax.axis_size("fsdp")
    pieces = share.reshape(share.shape[0], shards, -1).transpose(1, 0, 2)
    result = jnp.sum(lax.all_to_all(pieces, "fsdp", 0, 0).astype(jnp.float32), axis=0)
    return (
        master_next,
        moment_one_next,
        moment_two_next,
        weight_half,
        steps_next,
        result.astype(jnp.bfloat16),
    )


def solution(mesh):
    in_specs = (
        P("dp", "fsdp"),
        P("dp", "fsdp"),
        P("fsdp", None),
        P("fsdp", None),
        P("fsdp", None),
        P(("fsdp", "dp"), None),
        P(),
        P(),
    )
    out_specs = (
        P("fsdp", None),
        P("fsdp", None),
        P("fsdp", None),
        P("fsdp", None),
        P(),
        P("dp", "fsdp"),
    )
    return jax.shard_map(local, mesh=mesh, in_specs=in_specs, out_specs=out_specs, check_vma=False)
```

profile of v0, /device:TPU:0, one launch (start us, length us, event | category | flops | bytes accessed | tf_op | source)
XLA Modules:
  0.0 180.5 jit_solution(914096782585376441)
XLA Ops:
  7.2 0.0 all-gather.3.cloned.1.call-start
  7.2 0.7 all-gather.3.cloned.1.call-update
  7.9 0.0 all-gather.5.cloned.1.call-start
  7.9 47.6 %all-gather.3.cloned.1.call-done = bf16[128,5120]{1,0:T(8,128)(2,1)} async-done(((bf16[128,640]{1,0:T(8,128)(2,1)}), bf16[128,5120]{1,0:T(8,128)(2,1)}) %all-gather.3.cloned.1.call-update) | async-done | bytes 1310736 | tf_op jit(solution)/shard_map/all_gather | solution.py:18
  55.5 0.0 all-gather.5.cloned.1.call-update
  55.5 39.6 %psum.7 = s32[16]{0:T(128)S(1)} all-reduce(s32[16]{0:T(128)} %bitcast.12), channel_id=1, replica_groups=mesh['fsdp'=8,'dp'=4] {'fsdp','dp'}, use_global_device_ids=true, to_apply=%region_0.0 | all-reduce | flops 16 | bytes 128 | tf_op jit(solution)/shard_map/psum | solution.py:20
  95.9 0.1 broadcast_in_dim.25
  95.9 0.1 broadcast_in_dim.26
  96.0 0.7 power_subtract_fusion.1
  96.7 0.1 broadcast_in_dim.28
  96.8 0.1 sub.28
  96.8 0.1 broadcast_in_dim.29
  96.9 0.1 sub.30
  97.0 8.2 %all_gather.9 = bf16[512,512]{1,0:T(8,128)(2,1)S(1)} all-gather(bf16[128,512]{1,0:T(8,128)(2,1)} %param.8), channel_id=1, replica_groups=mesh['fsdp'=8,'dp'=4] {'dp'}, dimensions={0}, use_global_device_ids=true | all-gather | bytes 655360 | tf_op jit(solution)/shard_map/all_gather | solution.py:16
  105.2 0.0 all-gather.5.cloned.1.call-done
  105.2 26.5 %fusion.3 = (bf16[512,5120]{1,0:T(8,128)(2,1)}, f32[512,5120]{1,0:T(8,128)}, f32[512,5120]{1,0:T(8,128)}, f32[512,5120]{1,0:T(8,128)}) fusion(f32[512,5120]{1,0:T(8,128)} %param.10, f32[5120]{0:T(1024)S(1)} %sub.30, f32[512,5120]{1,0:T(8,128)} %param.12, f32[5120]{0:T(1024)S(1)} %sub.28, f32[512,5120]{1,0:T(8,128)} %param.11, f32[]{:T(128)} %bitcast.11, ...), kind=kOutput, calls=%fused_computation.11 | convolution fusion | flops 2728919040 | bytes 73970688 | tf_op jit(solution)/shard_map/dot_general | solution.py:21
  131.7 0.0 copy-done
  131.7 5.2 %convolution_convert_fusion = bf16[5120,128]{1,0:T(8,128)(2,1)} fusion(bf16[512,5120]{1,0:T(8,128)(2,1)} %get-tuple-element.12, bf16[128,512]{1,0:T(8,128)(2,1)S(1)} %copy-done), kind=kOutput, calls=%fused_computation.6 | convolution fusion | flops 671744000 | bytes 6684672 | tf_op jit(solution)/shard_map/dot_general | solution.py:35
  136.8 3.9 %all-to-all-start = ((bf16[8,128,640]{1,2,0:T(8,128)(2,1)}), bf16[8,128,640]{1,2,0:T(8,128)(2,1)S(1)}, u32[]{:S(2)}, u32[]{:S(2)}) async-start(bf16[8,128,640]{1,2,0:T(8,128)(2,1)} %bitcast.4), calls=%async_computation | async-start | bytes 2621440 | tf_op jit(solution)/shard_map/all_to_all | solution.py:40
  140.7 0.0 copy-done.1
  140.7 0.5 convert_add_fusion
  141.2 31.4 %all-to-all-done = bf16[8,128,640]{1,2,0:T(8,128)(2,1)S(1)} async-done(((bf16[8,128,640]{1,2,0:T(8,128)(2,1)}), bf16[8,128,640]{1,2,0:T(8,128)(2,1)S(1)}, u32[]{:S(2)}, u32[]{:S(2)}) %all-to-all-start) | async-done | bytes 1310752 | tf_op jit(solution)/shard_map/all_to_all | solution.py:40
  172.6 0.2 reduce_sum.12
  172.8 0.8 copy.14
  (3 shorter events, 0.0 us)
Async XLA Ops:
  7.2 48.3 %all-gather.3.cloned.1.call-start = ((), (), s32[]{:S(2)}) async-start(), calls=%async_computation.1 | async-start | bytes 1474560 | tf_op jit(solution)/shard_map/all_gather | solution.py:18
  7.9 97.3 %all-gather.5.cloned.1.call-start = ((), (), s32[]{:S(2)}) async-start(), calls=%async_computation.2 | async-start | bytes 6553600 | tf_op jit(solution)/shard_map/all_gather | solution.py:17
  105.2 26.5 %copy-start = (bf16[128,512]{1,0:T(8,128)(2,1)S(1)}, bf16[128,512]{1,0:T(8,128)(2,1)}, u32[]{:S(2)}) copy-start(bf16[128,512]{1,0:T(8,128)(2,1)} %param.8) | copy-start | bytes 393220
  105.2 35.6 %copy-start.1 = (s32[16]{0:T(128)S(1)}, s32[16]{0:T(128)}, u32[]{:S(2)}) copy-start(s32[16]{0:T(128)} %param.14) | copy-start | bytes 196
  136.8 35.8 %all-to-all-start = ((bf16[8,128,640]{1,2,0:T(8,128)(2,1)}), bf16[8,128,640]{1,2,0:T(8,128)(2,1)S(1)}, u32[]{:S(2)}, u32[]{:S(2)}) async-start(bf16[8,128,640]{1,2,0:T(8,128)(2,1)} %bitcast.4), calls=%async_computation | async-start | bytes 2621440 | tf_op jit(solution)/shard_map/all_to_all | solution.py:40
Sparse Core Ops, SparseCore 0:
  10.2 45.2 all-gather.2
  57.1 39.8 all-gather.4
where the time goes:
time: 181 us; the launch traced here: 180 us
  waiting for transfers between devices  79.6 us (44%)
  blocking collectives  47.8 us (26%)
  matrix products  31.7 us (18%)
  between operations  14.7 us (8%)
  starting transfers between devices  3.94 us (2%)
    all_gather x1, waiting for transfers between devices, local(): lax.all_gather(out_grad, 'fsdp', axis=1, tiled=True)  47.6 us
    psum x1, blocking collectives, local(): counts = lax.psum(flags[0], ('fsdp', 'dp'))  39.6 us
    all_to_all x1, waiting for transfers between devices, local(): lax.all_to_all(pieces, 'fsdp', 0, 0).astype(jnp.float32)  31.4 us
    dot_general x1, matrix products, local(): lax.dot_general(rows, grads, contract_rows, preferred_element_type=jnp.fl...  26.5 us
    all_gather x1, blocking collectives, local(): rows = lax.all_gather(tokens, 'dp', axis=0, tiled=True)  8.16 us
    dot_general x1, matrix products, local(): lax.dot_general(tokens, weight_half, (((1,), (0,)), ((), ())), preferred_...  5.16 us
    all_to_all x1, starting transfers between devices, local(): lax.all_to_all(pieces, 'fsdp', 0, 0).astype(jnp.float32)  3.87 us
  transfers between devices with their start and end apart: 3, of which 2 were waited for; matrix products, arithmetic and copies ran while one was open for 1% of the time, Pallas kernels for 0%

commit v1 on v0

--- a/solution.py
+++ b/solution.py
@@ -14,9 +14,17 @@
     bucket_width = width_out // BUCKETS
     contract_rows = (((0,), (0,)), ((), ()))
     rows = lax.all_gather(tokens, "dp", axis=0, tiled=True)
-    grads = lax.all_gather(
-        lax.all_gather(out_grad, "fsdp", axis=1, tiled=True), "dp", axis=0, tiled=True
-    )
+
+    def settle_units_up(sheet):
+        line_up = []
+        for _ in range(lax.axis_size("fsdp")):
+            line_up.append(sheet)
+        return jnp.concatenate(
+            lax.all_to_all(jnp.stack(line_up), axis_name="fsdp", split_axis=0, concat_axis=0),
+            axis=1,
+        )
+
+    grads = lax.all_gather(settle_units_up(out_grad), "dp", axis=0, tiled=True)
     counts = lax.psum(flags[0], ("fsdp", "dp"))
     gradient = lax.dot_general(rows, grads, contract_rows, preferred_element_type=jnp.float32)
     commit_bucket = counts == 0

time: 181 us -> 172 us (0.950)
  waiting for transfers between devices: 79.6 us -> 31.4 us
  blocking collectives: 47.8 us -> 86.6 us
    all_gather x2 -> x1, waiting for transfers between devices: 47.6 us -> 0.01 us  [local(): grads = lax.all_gather(settle_units_up(out_grad), 'dp', axis=0, tiled=True)]
    all_to_all x0 -> x1, blocking collectives: none -> 38.6 us  [settle_units_up(): lax.all_to_all(jnp.stack(line_up), axis_name='fsdp', split_axis=0, concat...]
  transfers between devices with their start and end apart: 3 -> 2, of which waited for: 2 -> 1; matrix products, arithmetic and copies ran while one was open for 1% -> 1% of each run, Pallas kernels for 0% -> 0%
where the time goes in v1:
time: 172 us
  blocking collectives  86.6 us (50%)
  waiting for transfers between devices  31.4 us (18%)
  matrix products  31.4 us (18%)
  between operations  14.7 us (9%)
  starting transfers between devices  3.85 us (2%)
  local copies, waits for them, and re-layouts  2.54 us (1%)
    psum x1, blocking collectives, local(): counts = lax.psum(flags[0], ('fsdp', 'dp'))  39.8 us
    all_to_all x1, blocking collectives, settle_units_up(): lax.all_to_all(jnp.stack(line_up), axis_name='fsdp', split_axis=0, concat...  38.6 us
    all_to_all x1, waiting for transfers between devices, local(): lax.all_to_all(pieces, 'fsdp', 0, 0).astype(jnp.float32)  31.4 us
    dot_general x1, matrix products, local(): lax.dot_general(rows, grads, contract_rows, preferred_element_type=jnp.fl...  26.3 us
    all_gather x1, blocking collectives, local(): rows = lax.all_gather(tokens, 'dp', axis=0, tiled=True)  8.16 us
    dot_general x1, matrix products, local(): lax.dot_general(tokens, weight_half, (((1,), (0,)), ((), ())), preferred_...  5.13 us
    all_to_all x1, starting transfers between devices, local(): lax.all_to_all(pieces, 'fsdp', 0, 0).astype(jnp.float32)  3.81 us
  transfers between devices with their start and end apart: 2, of which 1 were waited for; matrix products, arithmetic and copies ran while one was open for 1% of the time, Pallas kernels for 0%

profile of v1, /device:TPU:0, one launch (start us, length us, event | category | flops | bytes accessed | tf_op | source)
XLA Modules:
  0.0 171.9 jit_solution(1600665184070423364)
XLA Ops:
  7.2 0.0 all-gather.2.cloned.1.call-start
  7.2 1.1 copy.15
  8.3 0.2 stack.2
  8.5 38.6 %all_to_all.10 = bf16[8,128,640]{1,2,0:T(8,128)(2,1)} all-to-all(bf16[8,128,640]{1,2,0:T(8,128)(2,1)S(1)} %stack.2), channel_id=1, replica_groups=mesh['fsdp'=8,'dp'=4] {'fsdp'}, dimensions={0} | all-to-all | bytes 2621440 | tf_op jit(solution)/shard_map/all_to_all | solution.py:23
  47.1 0.0 all-gather.2.cloned.1.call-update
  47.1 39.8 %psum.7 = s32[16]{0:T(128)S(1)} all-reduce(s32[16]{0:T(128)} %bitcast.16), channel_id=1, replica_groups=mesh['fsdp'=8,'dp'=4] {'fsdp','dp'}, use_global_device_ids=true, to_apply=%region_0.0 | all-reduce | flops 16 | bytes 128 | tf_op jit(solution)/shard_map/psum | solution.py:28
  87.6 0.1 broadcast_in_dim.25
  87.7 0.1 broadcast_in_dim.26
  87.8 0.7 power_subtract_fusion.1
  88.4 0.1 broadcast_in_dim.28
  88.5 0.1 sub.28
  88.6 0.1 broadcast_in_dim.29
  88.7 0.1 sub.30
  88.7 8.2 %all_gather.6 = bf16[512,512]{1,0:T(8,128)(2,1)S(1)} all-gather(bf16[128,512]{1,0:T(8,128)(2,1)} %param.8), channel_id=1, replica_groups=mesh['fsdp'=8,'dp'=4] {'dp'}, dimensions={0}, use_global_device_ids=true | all-gather | bytes 655360 | tf_op jit(solution)/shard_map/all_gather | solution.py:16
  96.9 0.0 all-gather.2.cloned.1.call-done
  96.9 26.3 %fusion.3 = (bf16[512,5120]{1,0:T(8,128)(2,1)}, f32[512,5120]{1,0:T(8,128)}, f32[512,5120]{1,0:T(8,128)}, f32[512,5120]{1,0:T(8,128)}) fusion(f32[512,5120]{1,0:T(8,128)} %param.10, f32[5120]{0:T(1024)S(1)} %sub.30, f32[512,5120]{1,0:T(8,128)} %param.12, f32[5120]{0:T(1024)S(1)} %sub.28, f32[512,5120]{1,0:T(8,128)} %param.11, f32[]{:T(128)} %bitcast.14, ...), kind=kOutput, calls=%fused_computation.11 | convolution fusion | flops 2728919040 | bytes 73970688 | tf_op jit(solution)/shard_map/dot_general | solution.py:29
  123.2 0.0 copy-done
  123.2 5.1 %convolution_convert_fusion = bf16[5120,128]{1,0:T(8,128)(2,1)} fusion(bf16[512,5120]{1,0:T(8,128)(2,1)} %get-tuple-element.12, bf16[128,512]{1,0:T(8,128)(2,1)S(1)} %copy-done), kind=kOutput, calls=%fused_computation.6 | convolution fusion | flops 671744000 | bytes 6684672 | tf_op jit(solution)/shard_map/dot_general | solution.py:43
  128.3 3.8 %all-to-all-start.1 = ((bf16[8,128,640]{1,2,0:T(8,128)(2,1)}), bf16[8,128,640]{1,2,0:T(8,128)(2,1)S(1)}, u32[]{:S(2)}, u32[]{:S(2)}) async-start(bf16[8,128,640]{1,2,0:T(8,128)(2,1)} %bitcast.6), calls=%async_computation.1 | async-start | bytes 2621440 | tf_op jit(solution)/shard_map/all_to_all | solution.py:48
  132.1 0.0 copy-done.1
  132.1 0.5 convert_add_fusion
  132.6 31.4 %all-to-all-done.1 = bf16[8,128,640]{1,2,0:T(8,128)(2,1)S(1)} async-done(((bf16[8,128,640]{1,2,0:T(8,128)(2,1)}), bf16[8,128,640]{1,2,0:T(8,128)(2,1)S(1)}, u32[]{:S(2)}, u32[]{:S(2)}) %all-to-all-start.1) | async-done | bytes 1310752 | tf_op jit(solution)/shard_map/all_to_all | solution.py:48
  164.0 0.2 reduce_sum.12
  164.2 0.8 copy.16
  (3 shorter events, 0.0 us)
Async XLA Ops:
  7.2 89.7 %all-gather.2.cloned.1.call-start = ((), (), s32[]{:S(2)}) async-start(), calls=%async_computation.2 | async-start | bytes 6553600 | tf_op jit(solution)/shard_map/all_gather | solution.py:27
  96.9 26.3 %copy-start = (bf16[128,512]{1,0:T(8,128)(2,1)S(1)}, bf16[128,512]{1,0:T(8,128)(2,1)}, u32[]{:S(2)}) copy-start(bf16[128,512]{1,0:T(8,128)(2,1)} %param.8) | copy-start | bytes 393220
  96.9 35.2 %copy-start.1 = (s32[16]{0:T(128)S(1)}, s32[16]{0:T(128)}, u32[]{:S(2)}) copy-start(s32[16]{0:T(128)} %param.14) | copy-start | bytes 196
  128.3 35.7 %all-to-all-start.1 = ((bf16[8,128,640]{1,2,0:T(8,128)(2,1)}), bf16[8,128,640]{1,2,0:T(8,128)(2,1)S(1)}, u32[]{:S(2)}, u32[]{:S(2)}) async-start(bf16[8,128,640]{1,2,0:T(8,128)(2,1)} %bitcast.6), calls=%async_computation.1 | async-start | bytes 2621440 | tf_op jit(solution)/shard_map/all_to_all | solution.py:48
Sparse Core Ops, SparseCore 0:
  47.2 40.7 all-gather.1
